TPU v7x, 256 devices: a whole 4x4x8 slice. The times are simulated.
256 devices in a mesh: dp: 256 (over y, x, z, core).
Axes of the slice: x: 4, y: 4, z: 8, core: 2. Of those that a mesh axis runs over, the one named last changes fastest.
Arguments:
- image_emb: bfloat16 [2048, 1152], P('dp'), may hold values from -0.4375 to 0.4375
- text_tokens: bfloat16 [65536, 1152], P('dp'), may hold values from -0.078125 to 0.078125
- caption_ids: int32 [65536], P('dp'), may hold values from 0 to 2047, as said below
- groups: int32 [2048], P('dp'), may hold values from 0 to 511
- text_gain: float32 [1152], replicated, may hold values from 0.5 to 1.5
- log_scale: float32 [1], replicated, may hold values from 2 to 3
- logit_bias: float32 [1], replicated, may hold values from -3 to -1
Outputs:
- image_grad: float32 [2048, 1152], P('dp')
- token_grad: float32 [65536, 1152], P('dp')
- gain_grad: float32 [1152], replicated
- scalars: float32 [3], replicated
Inputs may be any that keep to these rules, and one draw needn't show every extreme that they name: `caption_ids`: caption ids never fall along the rows and every caption 0 .. 2047 has at least one row; the captions of the pairs of device d (ids 8 d to 8 (d + 1) - 1) all begin within the 256 rows of device d; the rows of device d before its first caption all belong to the last caption of device d - 1; device 0 begins with caption 0. `groups`: group ids of the pairs; equal ids mark matching pairs.
All inputs are finite; a program needn't handle non-finite values.
Results may differ from a plain program's by a relative error of at most 0.005.
Values may be sent and summed in bfloat16 or wider, within the bound.
No kernel may reach another device: no remote copies, remote signals or barrier semaphores. Data moves between devices by JAX's collectives and lax.ppermute only.
A program may use at most 64 MiB of HBM per device.

v0:
```python
import jax
import jax.numpy as jnp
from jax import lax
from jax.sharding import Mesh
from jax.sharding import PartitionSpec as P

DP = ("dp_0", "dp_1", "dp_2", "dp_3")


def from_behind(value, axis, by):
    count = lax.axis_size(axis)
    pairs = [(i, i + by) for i in range(count) if 0 <= i + by < count]
    return lax.ppermute(value, axis, pairs)


def side_by_side(arrays, axis, dim, along):
    ends, at = ([], 0)
    for a in arrays[:-1]:
        at += a.shape[along]
        ends.append(at)
    both = jnp.concatenate(arrays, axis=along)
    return tuple(jnp.split(lax.all_gather(both, axis, axis=dim, tiled=True), ends, axis=along))


def over_axes(value, axes):
    for axis in axes:
        value = lax.psum(value, axis)
    return value


def unit_rows(values):
    length = jnp.sqrt(jnp.sum(values * values, axis=1, keepdims=True))
    return (values / length, length)


def pair_margin(scaled, bias_value, row_groups, column_groups):
    labels = jnp.where(row_groups[:, None] == column_groups[None, :], 1.0, -1.0).astype(jnp.float32)
    margin = -labels * (scaled + bias_value)
    coeffs = -labels * jax.nn.sigmoid(margin)
    return (margin, coeffs)


def per_device(image_emb, text_tokens, caption_ids, groups, text_gain, log_scale, logit_bias):
    pairs_here = image_emb.shape[0]
    width_features = image_emb.shape[1]
    devices = lax.axis_size(DP)
    total_pairs = pairs_here * devices
    first_pair = lax.axis_index(DP) * pairs_here
    raw_image = image_emb.astype(jnp.float32)
    unit_image, image_norm = unit_rows(raw_image)
    image_low = unit_image.astype(jnp.bfloat16)
    local_ids = caption_ids - first_pair
    slot_index = lax.broadcasted_iota(jnp.int32, (1, pairs_here), 1)
    member = (local_ids[:, None] == slot_index).astype(jnp.bfloat16)
    pooled = lax.dot_general(
        member, text_tokens, (((0,), (0,)), ((), ())), preferred_element_type=jnp.float32
    )
    spilled = (local_ids == -1).astype(jnp.bfloat16)[None, :]
    spill_part = jnp.dot(spilled, text_tokens, preferred_element_type=jnp.float32)
    arrived = from_behind(spill_part, DP, -1)
    pooled = pooled.at[pairs_here - 1].add(arrived[0])
    embedded = pooled * text_gain[None, :]
    unit_text, text_norm = unit_rows(embedded)
    text_low = unit_text.astype(jnp.bfloat16)
    all_groups = lax.all_gather(groups, DP, axis=0, tiled=True)
    scale_value = jnp.exp(log_scale[0])
    bias_value = logit_bias[0]
    stored_width = 0
    initial = (
        jnp.zeros((pairs_here, width_features), jnp.float32),
        jnp.zeros((3,), jnp.float32),
        jnp.zeros((pairs_here, stored_width), jnp.bfloat16),
        jnp.zeros((pairs_here, width_features), jnp.float32),
    )
    block_rows, block_images = side_by_side((text_low, image_low), DP, 0, 1)
    scaled = scale_value * lax.dot_general(
        image_low, block_rows, (((1,), (1,)), ((), ())), preferred_element_type=jnp.float32
    )
    margin, coeffs = pair_margin(scaled, bias_value, groups, all_groups)
    coeff_low = coeffs.astype(jnp.bfloat16)
    image_acc = jnp.dot(coeff_low, block_rows, preferred_element_type=jnp.float32)
    sum_terms = jnp.stack(
        [jnp.sum(jax.nn.softplus(margin)), jnp.sum(coeffs * scaled), jnp.sum(coeffs)]
    )
    stored = initial[2]
    back_scaled = scale_value * lax.dot_general(
        block_images, text_low, (((1,), (1,)), ((), ())), preferred_element_type=jnp.float32
    )
    back_margin, back_coeffs = pair_margin(back_scaled, bias_value, all_groups, groups)
    back_low = back_coeffs.astype(jnp.bfloat16)
    carried = lax.dot_general(
        back_low, block_images, (((0,), (0,)), ((), ())), preferred_element_type=jnp.float32
    )
    image_acc, sum_terms, stored, carried = (image_acc, sum_terms, stored, carried)
    image_unit_grad = scale_value * image_acc
    text_unit_grad = scale_value * carried
    image_grad = (
        image_unit_grad - unit_image * jnp.sum(unit_image * image_unit_grad, axis=1, keepdims=True)
    ) / image_norm
    embed_grad = (
        text_unit_grad - unit_text * jnp.sum(unit_text * text_unit_grad, axis=1, keepdims=True)
    ) / text_norm
    gain_part = jnp.sum(embed_grad * pooled, axis=0)
    pooled_grad = embed_grad * text_gain[None, :]
    behind = from_behind(pooled_grad[pairs_here - 1 :], DP, 1)
    grad_table = jnp.concatenate([behind, pooled_grad], axis=0)
    token_grad = jnp.take(grad_table, local_ids + 1, axis=0)
    sum_terms, gain_grad = (over_axes(sum_terms, DP), over_axes(gain_part, DP))
    scalars = sum_terms / float(total_pairs * total_pairs)
    return (image_grad, token_grad, gain_grad, scalars)


def solution(mesh):
    finer = Mesh(mesh.devices.reshape(4, 4, 8, 2), ("dp_0", "dp_1", "dp_2", "dp_3"))
    placed = (P(DP, None), P(DP, None), P(DP), P(DP), P(), P(), P())
    return jax.shard_map(
        per_device,
        mesh=finer,
        in_specs=placed,
        out_specs=(P(DP, None), P(DP, None), P(), P()),
        check_vma=False,
    )
```

profile of v0, /device:TPU:1, one launch (start us, length us, event | category | flops | bytes accessed | tf_op | source)
XLA Modules:
  0.0 208.8 jit_solution(15179221970684075022)
XLA Ops:
  7.2 0.7 compare_and_fusion
  8.0 0.3 copy-done
  8.4 5.1 %collective-permute-start = (f32[1,1152]{1,0:T(1,128)S(1)}, f32[1,1152]{1,0:T(1,128)S(1)}, u32[]{:S(2)}, u32[]{:S(2)}) collective-permute-start(f32[1,1152]{1,0:T(1,128)S(1)} %fusion.67), channel_id=1, source_target_pairs={{1,0},{2,1},{3,2},{4,3},{5,4},{6,5},{7,6},{8,7},{9,8},{10,9},{11,1... | collective-permute-start | bytes 13832 | tf_op jit(solution)/shard_map/ppermute | solution.py:13
  13.6 0.3 fusion.55
  13.9 0.9 fusion.58
  14.9 0.8 multiply_reduce_fusion.4
  15.7 0.8 fusion.62
  16.5 0.6 pad_maximum_fusion.1
  18.5 0.9 dynamic-update-slice.3
  19.4 83.6 %all-reduce = s32[2048]{0:T(1024)S(1)} all-reduce(s32[2048]{0:T(1024)S(1)} %dynamic-update-slice.3), channel_id=1, replica_groups=mesh['dp_0'=4,'dp_1'=4,'dp_2'=8,'dp_3'=2] {'dp_0','dp_1','dp_2','dp_3'}, use_global_device_ids=true, to_apply=%add | all-reduce | flops 2048 | bytes 16384
  103.0 37.6 %all-gather.2.cloned.1.call-done = bf16[2048,2304]{1,0:T(8,128)(2,1)} async-done(((bf16[8,2304]{1,0:T(8,128)(2,1)}), bf16[2048,2304]{1,0:T(8,128)(2,1)}) %all-gather.2.cloned.1.call-update) | async-done | bytes 9437200 | tf_op jit(solution)/shard_map/all_gather | solution.py:22
  140.6 6.7 %multiply_reduce_fusion.2 = (f32[8]{0:T(128)S(1)}, f32[8,1152]{1,0:T(8,128)S(1)}) fusion(f32[8]{0:T(128)S(1)} %sqrt.17, f32[8,1152]{1,0:T(8,128)S(1)} %scatter-add.4, f32[1152]{0:T(1024)} %param.13, bf16[2048,2304]{1,0:T(8,128)(2,1)} %all-gather.2.cloned.1.call-done, bf16[8,1152]{1,0:T(8,128)(2,1)S(1)} %get-tuple-element.37, f32[]{:T(128)} %bitcast.11, ...), kind=kOutput, calls=%fused_computation.47 | convolution fusion | flops 75723768 | bytes 9547840 | tf_op jit(solution)/shard_map/dot_general | solution.py:91
  147.4 2.8 %collective-permute-start.1 = (f32[1,1152]{1,0:T(1,128)S(1)}, f32[1,1152]{1,0:T(1,128)S(1)}, u32[]{:S(2)}, u32[]{:S(2)}) collective-permute-start(f32[1,1152]{1,0:T(1,128)S(1)} %slice.25), channel_id=1, source_target_pairs={{0,1},{1,2},{2,3},{3,4},{4,5},{5,6},{6,7},{7,8},{8,9},{9,10},{10,1... | collective-permute-start | bytes 13832 | tf_op jit(solution)/shard_map/ppermute | solution.py:13
  150.3 4.4 %fusion.56 = (f32[]{:T(128)}, f32[]{:T(128)}, f32[]{:T(128)}, f32[8,2048]{1,0:T(8,128)S(1)}) fusion(f32[]{:T(128)} %bitcast.12, s32[2048]{0:T(1024)S(1)} %all-reduce, s32[8]{0:T(128)S(1)} %copy-done.3, bf16[8,1152]{1,0:T(8,128)(2,1)S(1)} %get-tuple-element.36, bf16[2048,2304]{1,0:T(8,128)(2,1)} %all-gather.2.cloned.1.call-done, f32[]{:T(128)} %bitcast), kind=kOutput, calls=%fused_computation.35 | convolution fusion | flops 38076416 | bytes 4811820 | tf_op jit(solution)/shard_map/dot_general | solution.py:76
  154.7 3.2 %multiply_reduce_fusion.3 = (f32[8]{0:T(128)S(1)}, f32[8,1152]{1,0:T(8,128)S(1)}) fusion(f32[8]{0:T(128)S(1)} %sqrt.16, bf16[8,1152]{1,0:T(8,128)(2,1)S(1)} %copy-done.1, bf16[2048,2304]{1,0:T(8,128)(2,1)} %all-gather.2.cloned.1.call-done, f32[8,2048]{1,0:T(8,128)S(1)} %get-tuple-element.35, f32[]{:T(128)} %bitcast.10, s32[2048]{0:T(1024)S(1)} %all-reduce, ...), kind=kOutput, calls=%fused_computation.49 | convolution fusion | flops 37958648 | bytes 4848736 | tf_op jit(solution)/shard_map/dot_general | solution.py:81
  157.9 0.7 subtract_divide_fusion.1
  158.6 2.0 pad_maximum_fusion.2
  160.6 9.1 %all-reduce.3 = (f32[1152]{0:T(1024)S(1)}, f32[3]{0:T(128)S(1)}) all-reduce(f32[1152]{0:T(1024)S(1)} %get-tuple-element.29, f32[3]{0:T(128)S(1)} %pad_maximum_fusion.2), channel_id=1, replica_groups=mesh['dp_0'=4,'dp_1'=4,'dp_2'=8,'dp_3'=2] {'dp_0'}, use_global_device_ids=true, to_apply=%region_5.6 | all-reduce | flops 1155 | bytes 9240 | tf_op jit(solution)/shard_map/psum | solution.py:27
  169.7 7.2 %all-reduce.2 = (f32[1152]{0:T(1024)S(1)}, f32[3]{0:T(128)S(1)}) all-reduce(f32[1152]{0:T(1024)S(1)} %get-tuple-element.23, f32[3]{0:T(128)S(1)} %get-tuple-element.24), channel_id=1, replica_groups=mesh['dp_0'=4,'dp_1'=4,'dp_2'=8,'dp_3'=2] {'dp_1'}, use_global_device_ids=true, to_apply=%region_6.7 | all-reduce | flops 1155 | bytes 9240 | tf_op jit(solution)/shard_map/psum | solution.py:27
  176.9 14.2 %all-reduce.1 = (f32[1152]{0:T(1024)S(1)}, f32[3]{0:T(128)S(1)}) all-reduce(f32[1152]{0:T(1024)S(1)} %get-tuple-element.21, f32[3]{0:T(128)S(1)} %get-tuple-element.22), channel_id=1, replica_groups=mesh['dp_0'=4,'dp_1'=4,'dp_2'=8,'dp_3'=2] {'dp_2'}, use_global_device_ids=true, to_apply=%region_7.8 | all-reduce | flops 1155 | bytes 9240 | tf_op jit(solution)/shard_map/psum | solution.py:27
  191.1 8.0 %all-reduce.4 = (f32[1152]{0:T(1024)}, f32[3]{0:T(128)S(1)}) all-reduce(f32[1152]{0:T(1024)S(1)} %get-tuple-element.19, f32[3]{0:T(128)S(1)} %get-tuple-element.20), channel_id=1, replica_groups=mesh['dp_0'=4,'dp_1'=4,'dp_2'=8,'dp_3'=2] {'dp_3'}, use_global_device_ids=true, to_apply=%region_8.9 | all-reduce | flops 1155 | bytes 9240 | tf_op jit(solution)/shard_map/psum | solution.py:27
  199.1 0.5 broadcast_multiply_fusion.1
  199.6 1.2 gather_fusion
  200.8 1.2 broadcast_select_fusion
  (24 shorter events, 0.6 us)
Async XLA Ops:
  7.2 1.1 copy-start
  7.2 133.4 %all-gather.2.cloned.1.call-start = ((), (), s32[]{:S(2)}) async-start(), calls=%async_computation | async-start | bytes 9474048 | tf_op jit(solution)/shard_map/all_gather | solution.py:22
  8.4 6.3 %collective-permute-start = (f32[1,1152]{1,0:T(1,128)S(1)}, f32[1,1152]{1,0:T(1,128)S(1)}, u32[]{:S(2)}, u32[]{:S(2)}) collective-permute-start(f32[1,1152]{1,0:T(1,128)S(1)} %fusion.67), channel_id=1, source_target_pairs={{1,0},{2,1},{3,2},{4,3},{5,4},{6,5},{7,6},{8,7},{9,8},{10,9},{11,1... | collective-permute-start | bytes 13832 | tf_op jit(solution)/shard_map/ppermute | solution.py:13
  140.6 6.7 %copy-start.2 = (f32[1152]{0:T(1024)S(1)}, f32[1152]{0:T(1024)}, u32[]{:S(2)}) copy-start(f32[1152]{0:T(1024)} %param.13) | copy-start | bytes 13828
  140.6 9.7 %copy-start.3 = (s32[8]{0:T(128)S(1)}, s32[8]{0:T(128)}, u32[]{:S(2)}) copy-start(s32[8]{0:T(128)} %param.12) | copy-start | bytes 100
  147.3 7.3 %copy-start.1 = (bf16[8,1152]{1,0:T(8,128)(2,1)S(1)}, bf16[8,1152]{1,0:T(8,128)(2,1)}, u32[]{:S(2)}) copy-start(bf16[8,1152]{1,0:T(8,128)(2,1)} %param.9) | copy-start | bytes 55300
  147.4 52.2 %collective-permute-start.1 = (f32[1,1152]{1,0:T(1,128)S(1)}, f32[1,1152]{1,0:T(1,128)S(1)}, u32[]{:S(2)}, u32[]{:S(2)}) collective-permute-start(f32[1,1152]{1,0:T(1,128)S(1)} %slice.25), channel_id=1, source_target_pairs={{0,1},{1,2},{2,3},{3,4},{4,5},{5,6},{6,7},{7,8},{8,9},{9,10},{10,1... | collective-permute-start | bytes 13832 | tf_op jit(solution)/shard_map/ppermute | solution.py:13
Sparse Core Ops, SparseCore 0:
  17.3 123.2 all-gather.1
where the time goes:
time: 209 us
  blocking collectives  122 us (58%)
  waiting for transfers between devices  37.6 us (18%)
  between operations  15.5 us (7%)
  matrix products  14.8 us (7%)
  other arithmetic  8.39 us (4%)
  starting transfers between devices  7.96 us (4%)
  local copies, waits for them, and re-layouts  2.51 us (1%)
    unnamed x1, blocking collectives  83.6 us
    psum x4, blocking collectives, over_axes(): value = lax.psum(value, axis)  38.5 us
    all_gather x1, waiting for transfers between devices, side_by_side(): lax.all_gather(both, axis, axis=dim, tiled=True)  37.6 us
    ppermute x2, starting transfers between devices, from_behind(): return lax.ppermute(value, axis, pairs)  7.93 us
    dot_general x1, matrix products, per_device(): lax.dot_general(back_low, block_images, (((0,), (0,)), ((), ())), preferr...  6.7 us
    dot_general x1, matrix products, per_device(): lax.dot_general(image_low, block_rows, (((1,), (1,)), ((), ())), preferre...  4.38 us
  transfers between devices with their start and end apart: 3, of which 1 were waited for; matrix products, arithmetic and copies ran while one was open for 6% of the time, Pallas kernels for 0%

commit v1 on v0

--- a/solution.py
+++ b/solution.py
@@ -24,7 +24,7 @@
 
 def over_axes(value, axes):
     for axis in axes:
-        value = lax.psum(value, axis)
+        value = jnp.sum(lax.all_gather(value, axis), axis=0)
     return value
 
 

time: 209 us -> 260 us (1.24)
  blocking collectives: 122 us -> 171 us
  waiting for transfers between devices: 37.6 us -> 30.1 us
  local copies, waits for them, and re-layouts: 2.51 us -> 8.71 us
  between operations: 15.5 us -> 18.1 us
    all_gather x0 -> x4, blocking collectives: none -> 45.3 us  [over_axes(): value = jnp.sum(lax.all_gather(value, axis), axis=0)]
    unnamed x1 -> x5, blocking collectives: 83.6 us -> 125 us
    psum x4 -> x0, blocking collectives: 38.5 us -> none  [over_axes(): value = lax.psum(value, axis)]
    all_gather x1, waiting for transfers between devices: 37.6 us -> 30.1 us  [side_by_side(): lax.all_gather(both, axis, axis=dim, tiled=True)]
    unnamed x10 -> x25, local copies, waits for them, and re-layouts: 1.15 us -> 7.01 us
  transfers between devices with their start and end apart: 3 -> 3, of which waited for: 1 -> 1; matrix products, arithmetic and copies ran while one was open for 6% -> 8% of each run, Pallas kernels for 0% -> 0%
where the time goes in v1:
time: 260 us; the launch traced here: 259 us
  blocking collectives  171 us (66%)
  waiting for transfers between devices  30.1 us (12%)
  between operations  18.1 us (7%)
  matrix products  14.1 us (5%)
  other arithmetic  9.3 us (4%)
  local copies, waits for them, and re-layouts  8.71 us (3%)
  starting transfers between devices  7.97 us (3%)
    unnamed x5, blocking collectives  125 us
    all_gather x4, blocking collectives, over_axes(): value = jnp.sum(lax.all_gather(value, axis), axis=0)  45.3 us
    all_gather x1, waiting for transfers between devices, side_by_side(): lax.all_gather(both, axis, axis=dim, tiled=True)  30.1 us
    ppermute x2, starting transfers between devices, from_behind(): return lax.ppermute(value, axis, pairs)  7.93 us
    unnamed x25, local copies, waits for them, and re-layouts  7.01 us
    dot_general x1, matrix products, per_device(): lax.dot_general(back_low, block_images, (((0,), (0,)), ((), ())), preferr...  6.04 us
  transfers between devices with their start and end apart: 3, of which 1 were waited for; matrix products, arithmetic and copies ran while one was open for 8% of the time, Pallas kernels for 0%

profile of v1, /device:TPU:1, one launch (start us, length us, event | category | flops | bytes accessed | tf_op | source)
XLA Modules:
  0.0 259.0 jit_solution(1743893375943543079)
XLA Ops:
  8.4 5.1 %collective-permute-start = (f32[1,1152]{1,0:T(1,128)S(1)}, f32[1,1152]{1,0:T(1,128)S(1)}, u32[]{:S(2)}, u32[]{:S(2)}) collective-permute-start(f32[1,1152]{1,0:T(1,128)S(1)} %fusion.67), channel_id=1, source_target_pairs={{1,0},{2,1},{3,2},{4,3},{5,4},{6,5},{7,6},{8,7},{9,8},{10,9},{11,1... | collective-permute-start | bytes 13832 | tf_op jit(solution)/shard_map/ppermute | solution.py:13
  13.9 0.9 fusion.52
  18.5 1.3 dynamic-slice.7
  19.8 1.3 dynamic-slice.8
  22.4 1.3 dynamic-slice.9
  24.3 1.3 dynamic-slice.10
  26.2 0.9 dynamic-update-slice.3
  27.1 83.3 %all-reduce = s32[2048]{0:T(1024)S(1)} all-reduce(s32[2048]{0:T(1024)S(1)} %dynamic-update-slice.3), channel_id=1, replica_groups=mesh['dp_0'=4,'dp_1'=4,'dp_2'=8,'dp_3'=2] {'dp_0','dp_1','dp_2','dp_3'}, use_global_device_ids=true, to_apply=%add | all-reduce | flops 2048 | bytes 16384
  110.4 30.1 %all-gather.14.cloned.1.call-done = bf16[2048,2304]{1,0:T(8,128)(2,1)} async-done(((bf16[8,2304]{1,0:T(8,128)(2,1)}), bf16[2048,2304]{1,0:T(8,128)(2,1)}) %all-gather.14.cloned.1.call-update) | async-done | bytes 9437200 | tf_op jit(solution)/shard_map/all_gather | solution.py:22
  140.5 6.0 %multiply_reduce_fusion.2 = (f32[8]{0:T(128)S(1)}, f32[8,1152]{1,0:T(8,128)S(1)}) fusion(f32[8]{0:T(128)S(1)} %sqrt.17, f32[8,1152]{1,0:T(8,128)S(1)} %scatter-add.4, f32[1152]{0:T(1024)} %param.13, bf16[2048,2304]{1,0:T(8,128)(2,1)} %all-gather.14.cloned.1.call-done, bf16[8,1152]{1,0:T(8,128)(2,1)S(1)} %get-tuple-element.29, f32[]{:T(128)} %bitcast.15, ...), kind=kOutput, calls=%fused_computation.41 | convolution fusion | flops 75723768 | bytes 9547840 | tf_op jit(solution)/shard_map/dot_general | solution.py:91
  146.7 2.8 %collective-permute-start.1 = (f32[1,1152]{1,0:T(1,128)S(1)}, f32[1,1152]{1,0:T(1,128)S(1)}, u32[]{:S(2)}, u32[]{:S(2)}) collective-permute-start(f32[1,1152]{1,0:T(1,128)S(1)} %slice.25), channel_id=1, source_target_pairs={{0,1},{1,2},{2,3},{3,4},{4,5},{5,6},{6,7},{7,8},{8,9},{9,10},{10,1... | collective-permute-start | bytes 13832 | tf_op jit(solution)/shard_map/ppermute | solution.py:13
  149.6 9.7 %all-gather.8 = f32[4,1,1152]{2,1,0:T(1,128)S(1)} all-gather(f32[1,1,1152]{2,1,0:T(1,128)S(1)} %reshape.89), channel_id=2, replica_groups=mesh['dp_0'=4,'dp_1'=4,'dp_2'=8,'dp_3'=2] {'dp_0'}, dimensions={0}, use_global_device_ids=true | all-gather | bytes 23040 | tf_op jit(solution)/shard_map/all_gather | solution.py:27
  159.2 4.4 %fusion.47 = (f32[]{:T(128)}, f32[]{:T(128)}, f32[]{:T(128)}, f32[8,2048]{1,0:T(8,128)S(1)}) fusion(f32[]{:T(128)} %bitcast.16, s32[2048]{0:T(1024)S(1)} %all-reduce, s32[8]{0:T(128)S(1)} %copy-done.3, bf16[8,1152]{1,0:T(8,128)(2,1)S(1)} %get-tuple-element.28, bf16[2048,2304]{1,0:T(8,128)(2,1)} %all-gather.14.cloned.1.call-done, f32[]{:T(128)} %bitcast), kind=kOutput, calls=%fused_computation.26 | convolution fusion | flops 38076416 | bytes 4811820 | tf_op jit(solution)/shard_map/dot_general | solution.py:76
  163.6 2.1 maximum_dynamic-update-slice_fusion
  165.8 8.0 %all-reduce.1 = f32[12]{0:T(128)S(1)} all-reduce(f32[12]{0:T(128)S(1)} %maximum_dynamic-update-slice_fusion), channel_id=6, replica_groups=mesh['dp_0'=4,'dp_1'=4,'dp_2'=8,'dp_3'=2] {'dp_0'}, use_global_device_ids=true, to_apply=%add.1 | all-reduce | flops 12 | bytes 96
  174.2 9.1 %all-gather.9 = f32[4,1,1152]{2,1,0:T(1,128)S(1)} all-gather(f32[1,1,1152]{2,1,0:T(1,128)S(1)} %reshape.91), channel_id=3, replica_groups=mesh['dp_0'=4,'dp_1'=4,'dp_2'=8,'dp_3'=2] {'dp_1'}, dimensions={0}, use_global_device_ids=true | all-gather | bytes 23040 | tf_op jit(solution)/shard_map/all_gather | solution.py:27
  183.3 6.8 %all-reduce.2 = f32[12]{0:T(128)S(1)} all-reduce(f32[12]{0:T(128)S(1)} %dynamic-update-slice.5), channel_id=7, replica_groups=mesh['dp_0'=4,'dp_1'=4,'dp_2'=8,'dp_3'=2] {'dp_1'}, use_global_device_ids=true, to_apply=%add.2 | all-reduce | flops 12 | bytes 96
  190.4 13.9 %all-reduce.3 = f32[24]{0:T(128)S(1)} all-reduce(f32[24]{0:T(128)S(1)} %dynamic-update-slice.6), channel_id=8, replica_groups=mesh['dp_0'=4,'dp_1'=4,'dp_2'=8,'dp_3'=2] {'dp_2'}, use_global_device_ids=true, to_apply=%add.3 | all-reduce | flops 24 | bytes 192
  204.7 13.3 %all-reduce.4 = f32[6]{0:T(128)S(1)} all-reduce(f32[6]{0:T(128)S(1)} %dynamic-update-slice.7), channel_id=9, replica_groups=mesh['dp_0'=4,'dp_1'=4,'dp_2'=8,'dp_3'=2] {'dp_3'}, use_global_device_ids=true, to_apply=%add.4 | all-reduce | flops 6 | bytes 48
  218.6 3.2 %multiply_reduce_fusion.3 = (f32[8]{0:T(128)S(1)}, f32[8,1152]{1,0:T(8,128)S(1)}) fusion(f32[8]{0:T(128)S(1)} %sqrt.16, bf16[8,1152]{1,0:T(8,128)(2,1)S(1)} %copy-done.1, bf16[2048,2304]{1,0:T(8,128)(2,1)} %all-gather.14.cloned.1.call-done, f32[8,2048]{1,0:T(8,128)S(1)} %get-tuple-element.27, f32[]{:T(128)} %bitcast.14, s32[2048]{0:T(1024)S(1)} %all-reduce, ...), kind=kOutput, calls=%fused_computation.43 | convolution fusion | flops 37958648 | bytes 4848736 | tf_op jit(solution)/shard_map/dot_general | solution.py:81
  222.6 18.5 %all-gather.10 = f32[8,1,1152]{2,1,0:T(1,128)S(1)} all-gather(f32[1,1,1152]{2,1,0:T(1,128)S(1)} %reshape.93), channel_id=4, replica_groups=mesh['dp_0'=4,'dp_1'=4,'dp_2'=8,'dp_3'=2] {'dp_2'}, dimensions={0}, use_global_device_ids=true | all-gather | bytes 41472 | tf_op jit(solution)/shard_map/all_gather | solution.py:27
  241.2 8.0 %all-gather.11 = f32[2,1,1152]{2,1,0:T(1,128)S(1)} all-gather(f32[1,1,1152]{2,1,0:T(1,128)S(1)} %reshape.95), channel_id=5, replica_groups=mesh['dp_0'=4,'dp_1'=4,'dp_2'=8,'dp_3'=2] {'dp_3'}, dimensions={0}, use_global_device_ids=true | all-gather | bytes 13824 | tf_op jit(solution)/shard_map/all_gather | solution.py:27
  249.8 1.2 gather_fusion
  251.0 1.2 broadcast_select_fusion
  (55 shorter events, 7.2 us)
Async XLA Ops:
  7.2 1.1 copy-start
  7.2 133.4 %all-gather.14.cloned.1.call-start = ((), (), s32[]{:S(2)}) async-start(), calls=%async_computation | async-start | bytes 9474048 | tf_op jit(solution)/shard_map/all_gather | solution.py:22
  8.4 6.3 %collective-permute-start = (f32[1,1152]{1,0:T(1,128)S(1)}, f32[1,1152]{1,0:T(1,128)S(1)}, u32[]{:S(2)}, u32[]{:S(2)}) collective-permute-start(f32[1,1152]{1,0:T(1,128)S(1)} %fusion.67), channel_id=1, source_target_pairs={{1,0},{2,1},{3,2},{4,3},{5,4},{6,5},{7,6},{8,7},{9,8},{10,9},{11,1... | collective-permute-start | bytes 13832 | tf_op jit(solution)/shard_map/ppermute | solution.py:13
  140.5 6.1 %copy-start.2 = (f32[1152]{0:T(1024)S(1)}, f32[1152]{0:T(1024)}, u32[]{:S(2)}) copy-start(f32[1152]{0:T(1024)} %param.13) | copy-start | bytes 13828
  140.5 18.7 %copy-start.3 = (s32[8]{0:T(128)S(1)}, s32[8]{0:T(128)}, u32[]{:S(2)}) copy-start(s32[8]{0:T(128)} %param.12) | copy-start | bytes 100
  146.6 72.1 %copy-start.1 = (bf16[8,1152]{1,0:T(8,128)(2,1)S(1)}, bf16[8,1152]{1,0:T(8,128)(2,1)}, u32[]{:S(2)}) copy-start(bf16[8,1152]{1,0:T(8,128)(2,1)} %param.9) | copy-start | bytes 55300
  146.7 103.1 %collective-permute-start.1 = (f32[1,1152]{1,0:T(1,128)S(1)}, f32[1,1152]{1,0:T(1,128)S(1)}, u32[]{:S(2)}, u32[]{:S(2)}) collective-permute-start(f32[1,1152]{1,0:T(1,128)S(1)} %slice.25), channel_id=1, source_target_pairs={{0,1},{1,2},{2,3},{3,4},{4,5},{5,6},{6,7},{7,8},{8,9},{9,10},{10,1... | collective-permute-start | bytes 13832 | tf_op jit(solution)/shard_map/ppermute | solution.py:13
Sparse Core Ops, SparseCore 0:
  17.3 123.2 all-gather.13
